TPU v7x, 32 devices: a whole 2x2x4 slice. The times are simulated.
32 devices in a mesh: freq: 4 (over x, core), rec: 8 (over z, y).
Axes of the slice: x: 2, y: 2, z: 4, core: 2. Of those that a mesh axis runs over, the one named last changes fastest.
Arguments:
- response_real: float32 [96, 1536, 1536], P('freq', 'rec'), may hold values from -0.109375 to 0.109375
- response_imaginary: float32 [96, 1536, 1536], P('freq', 'rec'), may hold values from -0.109375 to 0.109375
- focus: float32 [1536, 96, 128], P('rec', 'freq'), may hold values from -6 to 6
- initial: float32 [1536, 96, 128], P('rec', 'freq'), may hold values from -6 to 6
- onset: int32 [1536, 64], P('rec'), may hold values from 24 to 167
Outputs:
- focus_next: float32 [1536, 96, 128], P('rec', 'freq')
All inputs are finite; a program needn't handle non-finite values.
Results may differ from a plain program's by a relative error of at most 0.0003.
Values sent between devices are 32-bit elements; how exact they have to be, the bound alone decides.
A program may use at most 192 MiB of HBM per device.

v0:
```python
import functools
import math

import jax
import jax.numpy as jnp
import numpy as np
from jax import lax
from jax.experimental import pallas as pl
from jax.experimental.pallas import tpu as pltpu
from jax.sharding import PartitionSpec as P

CORES = 2
SUBS = 2
VMEM_LIMIT = 63 * 2**20
MESH = pl.DeviceIdType.MESH
ANY = pl.BlockSpec(memory_space=pl.ANY)
IN_VMEM = pl.BlockSpec(memory_space=pltpu.VMEM)


class Place:
    def __init__(self):
        total = lax.axis_size("rec")
        ys = 1 << ((total.bit_length() - 1) // 2)
        self.Y = ys if total % ys == 0 else 1
        self.Z = total // self.Y
        self.FQ = lax.axis_size("freq")
        self.X = self.FQ // CORES
        self.rec = lax.axis_index("rec")
        self.freq = lax.axis_index("freq")
        self.z, self.y = self.rec // self.Y, self.rec % self.Y
        self.x, self.c = self.freq // CORES, self.freq % CORES
        self.down_hops, self.up_hops = self.Z - 1 - self.z, self.z
        self.bottom, self.top = self.z == 0, self.z == self.Z - 1
        self.corner = jnp.logical_or(self.bottom, self.top)
        self.end = jnp.where(self.bottom, 0, 1)
        self.unit = self.end * self.Y + self.y

    def above(self):
        return (self.freq, self.rec + self.Y)

    def below(self):
        return (self.freq, self.rec - self.Y)

    def beside(self, dy):
        return (self.freq, self.z * self.Y + (self.y + dy) % self.Y)


def remote(src, dst, send, recv, device):
    return pltpu.make_async_remote_copy(src, dst, send, recv, device_id=device, device_id_type=MESH)


def within(k, count):
    return jnp.logical_and(k >= 0, k < count)


def both(a, b):
    return jnp.logical_and(a, b)


def split(x):
    high = x.astype(jnp.bfloat16)
    return high, (x - high.astype(jnp.float32)).astype(jnp.bfloat16)


def loop(count, body):
    lax.fori_loop(0, count, lambda k, _: (body(k), 0)[1], 0)


def fetch_response(real_ref, imag_ref, buf, sems, f):
    slots = buf.shape[0]
    rows = buf.shape[1] // 2
    slot = f % slots
    return [
        pltpu.make_async_copy(ref.at[f], buf.at[slot, pl.ds(k * rows, rows)], sems.at[slot, k])
        for k, ref in enumerate((real_ref, imag_ref))
    ]


def spread(p, f, half, src, dst, own_sem, send, recv):
    nf = dst.shape[0] // p.FQ
    row = p.freq * nf + f
    for dx in range(p.X):
        target = ((p.x + dx) % p.X * CORES + half, p.rec)
        copy = remote(src, dst.at[row], send.at[half, dx, f], recv.at[p.freq, f], target)
        if dx == 0:
            mine = p.c == half

            @pl.when(mine)
            def _():
                pltpu.make_async_copy(src, dst.at[row], own_sem.at[f]).start()

            @pl.when(jnp.logical_not(mine))
            def _():
                copy.start()
        else:
            copy.start()


def spread_wait(p, f, src, dst, own_sem, send, recv):
    nf = dst.shape[0] // p.FQ
    pltpu.make_async_copy(src, dst.at[p.freq * nf + f], own_sem.at[f]).wait()
    for half in range(CORES):
        for dx in range(p.X):
            copy = remote(src, dst.at[f], send.at[half, dx, f], recv.at[p.freq, f], (p.freq, p.rec))
            if dx == 0:

                @pl.when(p.c != half)
                def _():
                    copy.wait_send()
            else:
                copy.wait_send()
    for source in range(p.FQ):

        @pl.when(p.freq != source)
        def _():
            remote(src, dst.at[source * nf + f], send.at[0, 0, f], recv.at[source, f], (p.freq, p.rec)).wait_recv()


def adjoint_kernel(focus_ref, onset_ref, real_ref, imag_ref, out_ref, own_onset_ref, *scratch):
    (term, buf, ry, rd1, ru1, rd2, ru2, rf) = scratch[:8]
    (fetch_sem, sy, qy, sd1, qd1, su1, qu1, sd2, qd2, su2, qu2, sf, qf, own_sem, sx, qx, so, qo) = scratch[8:]
    p = Place()
    nf, _, Y, SU, width = term.shape
    slots = buf.shape[0]
    pairs = nf // 2
    count = pairs * SUBS
    SR, SH = SU // SUBS, SU // CORES
    H = p.Z // 2
    U = 2 * Y
    nr = buf.shape[1] // 2
    sign = jnp.where(lax.broadcasted_iota(jnp.int32, (1, width), 1) < width // 2, 1.0, -1.0)

    def fetch(f):
        return fetch_response(real_ref, imag_ref, buf, fetch_sem, f)

    for f in range(min(slots, nf)):
        for copy in fetch(f):
            copy.start()

    owner = p.rec // H
    owner_rec = owner // Y * (p.Z - 1) * Y + owner % Y
    onset_rows = onset_ref.shape[0]

    def onset_copy(at):
        dst = own_onset_ref.at[pl.ds(at * onset_rows, onset_rows)]
        return remote(onset_ref, dst, so.at[0], qo.at[at], (p.freq, owner_rec))

    @pl.when(owner_rec == p.rec)
    def _():
        at = p.rec % H
        pltpu.make_async_copy(onset_ref, own_onset_ref.at[pl.ds(at * onset_rows, onset_rows)], so.at[1]).start()

    @pl.when(owner_rec != p.rec)
    def _():
        onset_copy(p.rec % H).start()

    def compute(f):
        for copy in fetch(f):
            copy.wait()
        slot = f % slots
        x = focus_ref[pl.ds(f, nr, stride=nf), :]
        crossed = pltpu.roll(x, width // 2, 1) * sign
        z_high, z_low = split(jnp.concatenate([x, crossed], axis=0).T)
        z = jnp.concatenate([z_high, z_low], axis=0)
        for u in range(0, U, 2):
            high, low = split(buf[slot, :, u * SU : (u + 2) * SU])
            wide = jnp.dot(z, high, preferred_element_type=jnp.float32)
            rest = jnp.dot(z_high, low, preferred_element_type=jnp.float32)
            total = wide[:width] + wide[width:] + rest
            term[f, u // Y, u % Y : u % Y + 2] = total.T.reshape(2, SU, width)

        @pl.when(f + slots < nf)
        def _():
            for copy in fetch(f + slots):
                copy.start()

    def rows_of(k):
        return pl.ds(k % SUBS * SR, SR)

    def halves(k):
        return range(CORES) if SUBS == 1 else [k % SUBS]

    def deliver(f, k):
        if SUBS == 1:
            for half in range(CORES):
                spread(p, f, half, term.at[f, p.end, p.y, pl.ds(half * SH, SH)], out_ref, own_sem, sx, qx)
        else:
            for half in range(CORES):

                @pl.when(k % SUBS == half)
                def _():
                    spread(p, f, half, term.at[f, p.end, p.y, pl.ds(half * SH, SH)], out_ref, own_sem, sx, qx)

    def y_copy(k, dy):
        f = k // SUBS * 2
        src = term.at[f, :, (p.y + dy) % Y, rows_of(k)]
        return remote(src, ry.at[k, dy - 1], sy.at[k, dy - 1], qy.at[k, dy - 1], p.beside(dy))

    def final_copy(k, dy):
        f = k // SUBS * 2 + 1
        src = term.at[f, p.end, (p.y + dy) % Y, rows_of(k)]
        return remote(src, rf.at[k, dy - 1], sf.at[k, dy - 1], qf.at[k, dy - 1], p.beside(dy))

    def wide_copy(k, end):
        f = k // SUBS * 2 + 1
        src = term.at[f, end, :, rows_of(k)]
        if end == 0:
            return remote(src, rd2.at[k], sd2.at[k], qd2.at[k], p.below())
        return remote(src, ru2.at[k], su2.at[k], qu2.at[k], p.above())

    def thin_copy(k, end):
        f = k // SUBS * 2
        src = term.at[f, end, p.y, rows_of(k)]
        if end == 0:
            return remote(src, rd1.at[k], sd1.at[k], qd1.at[k], p.below())
        return remote(src, ru1.at[k], su1.at[k], qu1.at[k], p.above())

    starts = (p.top, p.bottom)
    stops = (p.bottom, p.top)
    hops = (p.down_hops, p.up_hops)
    thin_from, wide_from = (rd1, ru1), (rd2, ru2)

    def step(i):
        if SUBS == 1:
            fresh = i < count
        else:
            fresh = both(i < count, i % SUBS == 0)

        @pl.when(fresh)
        def _():
            f = i // SUBS * 2
            compute(f)
            compute(f + 1)

        @pl.when(i < count)
        def _():
            for dy in range(1, Y):
                y_copy(i, dy).start()
            for end in range(2):

                @pl.when(starts[end])
                def _():
                    wide_copy(i, end).start()

        for end in range(2):
            k = i - hops[end]

            @pl.when(both(jnp.logical_not(starts[end]), within(k, count)))
            def _():
                f = k // SUBS * 2 + 1
                wide_copy(k, end).wait_recv()
                term[f, end, :, rows_of(k)] += wide_from[end][k]

                @pl.when(jnp.logical_not(stops[end]))
                def _():
                    wide_copy(k, end).start()

                @pl.when(stops[end])
                def _():
                    for dy in range(1, Y):
                        final_copy(k, dy).start()

        @pl.when(within(i - 1, count))
        def _():
            k = i - 1
            f = k // SUBS * 2
            for dy in range(1, Y):
                y_copy(k, dy).wait_recv()
                term[f, :, p.y, rows_of(k)] += ry[k, dy - 1]
            for end in range(2):

                @pl.when(starts[end])
                def _():
                    thin_copy(k, end).start()

        for end in range(2):
            k = i - 1 - hops[end]

            @pl.when(both(jnp.logical_not(starts[end]), within(k, count)))
            def _():
                f = k // SUBS * 2
                thin_copy(k, end).wait_recv()
                term[f, end, p.y, rows_of(k)] += thin_from[end][k]

                @pl.when(jnp.logical_not(stops[end]))
                def _():
                    thin_copy(k, end).start()

                @pl.when(stops[end])
                def _():
                    deliver(f, k)

        @pl.when(both(p.corner, within(i - p.Z, count)))
        def _():
            k = i - p.Z
            f = k // SUBS * 2 + 1
            for dy in range(1, Y):
                final_copy(k, dy).wait_recv()
                term[f, p.end, p.y, rows_of(k)] += rf[k, dy - 1]
            deliver(f, k)

    loop(count + p.Z, step)

    def finish(k):
        for dy in range(1, Y):
            y_copy(k, dy).wait_send()
        for end in range(2):

            @pl.when(jnp.logical_not(stops[end]))
            def _():
                wide_copy(k, end).wait_send()
                thin_copy(k, end).wait_send()

        @pl.when(p.corner)
        def _():
            for dy in range(1, Y):
                final_copy(k, dy).wait_send()

    loop(count, finish)

    @pl.when(p.corner)
    def _():
        loop(nf, lambda f: spread_wait(p, f, term.at[f, p.end, p.y, pl.ds(0, SH)], out_ref, own_sem, sx, qx))
        for at in range(H):

            @pl.when(p.unit * H + at != p.rec)
            def _():
                onset_copy(at).wait_recv()

    @pl.when(owner_rec == p.rec)
    def _():
        pltpu.make_async_copy(onset_ref, own_onset_ref.at[pl.ds(0, onset_rows)], so.at[1]).wait()

    @pl.when(owner_rec != p.rec)
    def _():
        onset_copy(0).wait_send()


def adjoint(focus, onset_pairs, real, imag):
    p = Place()
    nf, nr, ns = real.shape
    width = focus.shape[2]
    Y, Z = p.Y, p.Z
    H = Z // 2
    SU = H * nr
    count = nf // 2 * SUBS
    SR, SH = SU // SUBS, SU // CORES
    f32 = jnp.float32
    dma = pltpu.SemaphoreType.DMA
    scratch = [
        pltpu.VMEM((nf, 2, Y, SU, width), f32),
        pltpu.VMEM((2, 2 * nr, ns), f32),
        pltpu.VMEM((count, Y - 1, 2, SR, width), f32),
        pltpu.VMEM((count, SR, width), f32),
        pltpu.VMEM((count, SR, width), f32),
        pltpu.VMEM((count, Y, SR, width), f32),
        pltpu.VMEM((count, Y, SR, width), f32),
        pltpu.VMEM((count, Y - 1, SR, width), f32),
        dma((2, 2)),
        dma((count, Y - 1)),
        dma((count, Y - 1)),
        *[dma((count,))] * 8,
        dma((count, Y - 1)),
        dma((count, Y - 1)),
        dma((nf,)),
        dma((CORES, p.X, nf)),
        dma((p.FQ, nf)),
        dma((2,)),
        dma((H,)),
    ]
    return pl.pallas_call(
        adjoint_kernel,
        out_shape=(
            jax.ShapeDtypeStruct((p.FQ * nf, SH, width), f32),
            jax.ShapeDtypeStruct((H * onset_pairs.shape[0], onset_pairs.shape[1]), jnp.int32),
        ),
        in_specs=[IN_VMEM, ANY, ANY, ANY],
        out_specs=(ANY, ANY),
        scratch_shapes=scratch,
        compiler_params=pltpu.CompilerParams(has_side_effects=True, vmem_limit_bytes=VMEM_LIMIT),
        name="adjoint",
    )(focus.reshape(nr * nf, width), onset_pairs, real, imag)


def forward_kernel(win_ref, real_ref, imag_ref, out_ref, *scratch):
    (full, buf, fo) = scratch[:3]
    (fetch_sem, s0, q0, l0, sy, qy, sd1, qd1, su1, qu1, sd2, qd2, su2, qu2, sf, qf, own_sem, sx, qx) = scratch[3:]
    p = Place()
    nf, _, Y, SU, width = full.shape
    slots = buf.shape[0]
    nr = buf.shape[1] // 2
    half_width = width // 2
    pairs = nf // 2
    count = pairs * SUBS
    SR, SH = SU // SUBS, SU // CORES
    NH = nr // CORES
    U = 2 * Y

    def fetch(f):
        return fetch_response(real_ref, imag_ref, buf, fetch_sem, f)

    for f in range(min(slots, nf)):
        for copy in fetch(f):
            copy.start()

    def own_copy(g):
        rows = pl.ds(p.c * SH, SH)
        return pltpu.make_async_copy(
            win_ref.at[p.c, pl.ds(2 * g, 2)], full.at[pl.ds(2 * g, 2), p.end, p.y, rows], l0.at[g]
        )

    def core_copy(g):
        rows = pl.ds(p.c * SH, SH)
        return remote(
            win_ref.at[1 - p.c, pl.ds(2 * g, 2)],
            full.at[pl.ds(2 * g, 2), p.end, p.y, rows],
            s0.at[g],
            q0.at[g],
            (p.x * CORES + 1 - p.c, p.rec),
        )

    @pl.when(p.corner)
    def _():
        def begin(g):
            core_copy(g).start()
            own_copy(g).start()

        loop(pairs, begin)

    def rows_of(k):
        return pl.ds(k % SUBS * SR, SR)

    def first_y(k, dy, end):
        src = full.at[k // SUBS * 2 + 1, end, p.y, rows_of(k)]
        return remote(src, src, sf.at[k, dy - 1], qf.at[k, dy - 1], p.beside(dy))

    def last_y(k, dy, end):
        src = full.at[k // SUBS * 2, end, p.y, rows_of(k)]
        return remote(src, src, sy.at[end, k, dy - 1], qy.at[end, k, dy - 1], p.beside(dy))

    def thin_copy(k, end):
        src = full.at[k // SUBS * 2, end, p.y, rows_of(k)]
        if end == 0:
            return remote(src, src, su1.at[k], qu1.at[k], p.above())
        return remote(src, src, sd1.at[k], qd1.at[k], p.below())

    def wide_copy(k, end):
        src = full.at[k // SUBS * 2 + 1, end, :, rows_of(k)]
        if end == 0:
            return remote(src, src, su2.at[k], qu2.at[k], p.above())
        return remote(src, src, sd2.at[k], qd2.at[k], p.below())

    starts = (p.bottom, p.top)
    stops = (p.top, p.bottom)
    hops = (p.up_hops, p.down_hops)

    def compute(f):
        for copy in fetch(f):
            copy.wait()
        slot = f % slots
        total = None
        for u in range(U):
            high, low = split(buf[slot, :, u * SU : (u + 1) * SU])
            f_high, f_low = split(full[f, u // Y, u % Y])
            wide = jnp.dot(
                high, jnp.concatenate([f_high, f_low], axis=1), preferred_element_type=jnp.float32
            )
            rest = jnp.dot(low, f_high, preferred_element_type=jnp.float32)
            piece = wide[:, :width] + wide[:, width:] + rest
            total = piece if total is None else total + piece
        turned = pltpu.roll(total[nr:], half_width, 1)
        lane = lax.broadcasted_iota(jnp.int32, (1, width), 1)
        fo[f] = total[:nr] + jnp.where(lane < half_width, -turned, turned)

        @pl.when(f + slots < nf)
        def _():
            for copy in fetch(f + slots):
                copy.start()

    def deliver(f):
        for half in range(CORES):
            spread(p, f, half, fo.at[f, pl.ds(half * NH, NH)], out_ref, own_sem, sx, qx)

    def step(i):
        @pl.when(both(p.corner, i < count))
        def _():
            if SUBS == 1:
                fresh = i >= 0
            else:
                fresh = i % SUBS == 0

            @pl.when(fresh)
            def _():
                own_copy(i // SUBS).wait()
                core_copy(i // SUBS).wait_recv()

            for end in range(2):

                @pl.when(starts[end])
                def _():
                    for dy in range(1, Y):
                        first_y(i, dy, end).start()

        for end in range(2):
            k = i - hops[end]

            @pl.when(within(k, count))
            def _():
                @pl.when(jnp.logical_not(starts[end]))
                def _():
                    thin_copy(k, end).wait_recv()

                @pl.when(jnp.logical_not(stops[end]))
                def _():
                    thin_copy(k, end).start()

                for dy in range(1, Y):
                    last_y(k, dy, end).start()

            j = i - 1 - hops[end]

            @pl.when(within(j, count))
            def _():
                @pl.when(starts[end])
                def _():
                    for dy in range(1, Y):
                        first_y(j, dy, end).wait_recv()

                @pl.when(jnp.logical_not(starts[end]))
                def _():
                    wide_copy(j, end).wait_recv()

                @pl.when(jnp.logical_not(stops[end]))
                def _():
                    wide_copy(j, end).start()

        k = i - p.Z

        @pl.when(within(k, count))
        def _():
            for end in range(2):
                for dy in range(1, Y):
                    last_y(k, dy, end).wait_recv()

            if SUBS == 1:
                ready = k >= 0
            else:
                ready = k % SUBS == SUBS - 1

            @pl.when(ready)
            def _():
                f = k // SUBS * 2
                compute(f)
                deliver(f)
                compute(f + 1)
                deliver(f + 1)

    loop(count + p.Z, step)

    def finish(k):
        for end in range(2):
            for dy in range(1, Y):
                last_y(k, dy, end).wait_send()

            @pl.when(jnp.logical_not(stops[end]))
            def _():
                thin_copy(k, end).wait_send()
                wide_copy(k, end).wait_send()

            @pl.when(starts[end])
            def _():
                for dy in range(1, Y):
                    first_y(k, dy, end).wait_send()

    loop(count, finish)

    @pl.when(p.corner)
    def _():
        loop(pairs, lambda g: core_copy(g).wait_send())

    loop(nf, lambda f: spread_wait(p, f, fo.at[f, pl.ds(0, NH)], out_ref, own_sem, sx, qx))


def forward(windowed, real, imag):
    p = Place()
    nf, nr, ns = real.shape
    width = windowed.shape[3]
    Y, Z = p.Y, p.Z
    SU = Z // 2 * nr
    count = nf // 2 * SUBS
    f32 = jnp.float32
    dma = pltpu.SemaphoreType.DMA
    scratch = [
        pltpu.VMEM((nf, 2, Y, SU, width), f32),
        pltpu.VMEM((4, 2 * nr, ns), f32),
        pltpu.VMEM((nf, nr, width), f32),
        dma((4, 2)),
        dma((nf // 2,)),
        dma((nf // 2,)),
        dma((nf // 2,)),
        dma((2, count, Y - 1)),
        dma((2, count, Y - 1)),
        *[dma((count,))] * 8,
        dma((count, Y - 1)),
        dma((count, Y - 1)),
        dma((nf,)),
        dma((CORES, p.X, nf)),
        dma((p.FQ, nf)),
    ]
    return pl.pallas_call(
        forward_kernel,
        out_shape=jax.ShapeDtypeStruct((p.FQ * nf, nr // CORES, width), f32),
        in_specs=[ANY, ANY, ANY],
        out_specs=ANY,
        scratch_shapes=scratch,
        compiler_params=pltpu.CompilerParams(has_side_effects=True, vmem_limit_bytes=VMEM_LIMIT),
        name="forward",
    )(windowed, real, imag)


def split_host(table):
    high = np.asarray(table, dtype=jnp.bfloat16)
    low = np.asarray(table - high.astype(np.float64), dtype=jnp.bfloat16)
    return high, low


def tables(freqs):
    samples = 2 * freqs
    order = np.arange(freqs)
    sample = np.arange(samples)
    phases = 2.0 * math.pi / samples * (order[:, None] * sample[None, :] % samples)
    cosine, sine = np.cos(phases), np.sin(phases)
    factor = np.where(order == 0, 1.0, 2.0)[:, None] / samples
    inverse = np.concatenate([(factor * cosine).T, (-factor * sine).T], axis=1)
    return (*split_host(inverse), *split_host(cosine), *split_host(-sine))


def triple(high, low, x):
    x_high, x_low = split(x)
    dot = functools.partial(jnp.dot, preferred_element_type=jnp.float32)
    return dot(high, x_high) + (dot(high, x_low) + dot(low, x_high))


def window_kernel(by_row, onset_ref, ih_ref, il_ref, fh_ref, fl_ref, x_ref, o_ref):
    freqs, rows, width = x_ref.shape
    samples = 2 * freqs
    half = width // 2
    kept = fh_ref.shape[0] // 2
    own = kept // CORES
    first = lax.broadcasted_iota(jnp.int32, (1, width), 1) < half
    sample = lax.broadcasted_iota(jnp.int32, (samples, width), 0)
    pairs = rows // 2
    packed = []
    for i in range(pairs):
        a, b = x_ref[:, 2 * i, :], x_ref[:, 2 * i + 1, :]
        real = jnp.where(first, a, pltpu.roll(b, half, 1))
        imag = jnp.where(first, pltpu.roll(a, half, 1), b)
        packed.append(jnp.concatenate([real, imag], axis=0))
    traces = triple(ih_ref[...], il_ref[...], jnp.concatenate(packed, axis=1))
    clipped = [
        jnp.where(sample < onset_ref[0, i : i + 1, :], traces[:, i * width : (i + 1) * width], 0.0)
        for i in range(pairs)
    ]
    back = triple(fh_ref[...], fl_ref[...], jnp.concatenate(clipped, axis=1))
    for i in range(pairs):
        real = back[:kept, i * width : (i + 1) * width]
        imag = back[kept:, i * width : (i + 1) * width]
        a = jnp.where(first, real, pltpu.roll(imag, half, 1))
        b = jnp.where(first, pltpu.roll(real, half, 1), imag)
        for n, value in ((2 * i, a), (2 * i + 1, b)):
            for core in range(CORES):
                piece = value[core * own : (core + 1) * own]
                if by_row:
                    o_ref[core, n] = piece
                else:
                    o_ref[core, :, n, :] = piece


def window(spectrum, onset_pairs, consts, by_row):
    freqs, count, width = spectrum.shape
    own = consts[2].shape[0] // 2 // CORES
    rows = 8
    onset_pairs = onset_pairs.reshape(count // rows, rows // 2, width)
    whole = [pl.BlockSpec(t.shape, lambda i: (0, 0)) for t in consts]
    if by_row:
        out_shape, out_block = (CORES, count, own, width), (CORES, rows, own, width)
        out_spec = pl.BlockSpec(out_block, lambda i: (0, i, 0, 0))
    else:
        out_shape, out_block = (CORES, own, count, width), (CORES, own, rows, width)
        out_spec = pl.BlockSpec(out_block, lambda i: (0, 0, i, 0))
    return pl.pallas_call(
        functools.partial(window_kernel, by_row),
        grid=(count // rows,),
        in_specs=[
            pl.BlockSpec((1, rows // 2, width), lambda i: (i, 0, 0)),
            *whole,
            pl.BlockSpec((freqs, rows, width), lambda i: (0, i, 0)),
        ],
        out_specs=out_spec,
        out_shape=jax.ShapeDtypeStruct(out_shape, jnp.float32),
        name="window_rows" if by_row else "window",
    )(onset_pairs, *consts, spectrum)


def on_device(response_real, response_imaginary, focus, initial, onset):
    p = Place()
    nf, nr, _ = response_real.shape
    width = focus.shape[2]
    onset_pairs = onset.reshape(nr // 2, width)

    inv_high, inv_low, cos_high, cos_low, sin_high, sin_low = tables(p.FQ * nf)

    def chip_rows(cosine, sine):
        at = p.x * CORES * nf
        cut = [lax.dynamic_slice_in_dim(jnp.asarray(t), at, CORES * nf, 0) for t in (cosine, sine)]
        return jnp.concatenate(cut, axis=0)

    consts = [jnp.asarray(inv_high), jnp.asarray(inv_low), chip_rows(cos_high, sin_high), chip_rows(cos_low, sin_low)]

    spectrum, own_onset = adjoint(focus, onset_pairs, response_real, response_imaginary)
    SH = spectrum.shape[1]
    mine = lax.dynamic_slice_in_dim(own_onset, p.c * (SH // 2), SH // 2, 0)
    windowed = window(spectrum, mine, consts, False)
    received = forward(windowed, response_real, response_imaginary)
    quarter = nr // CORES // 2
    mine = lax.dynamic_slice_in_dim(onset_pairs, p.c * quarter, quarter, 0)
    update = window(received, mine, consts, True)
    keep = lax.dynamic_index_in_dim(update, p.c, 0, keepdims=False)
    give = lax.dynamic_index_in_dim(update, 1 - p.c, 0, keepdims=False)
    swap = [(i, i ^ 1) for i in range(p.FQ)]
    got = lax.ppermute(give, "freq", swap)
    low = jnp.where(p.c == 0, keep, got)
    high = jnp.where(p.c == 0, got, keep)
    return initial - jnp.concatenate([low, high], axis=0)


def solution(mesh):
    return jax.shard_map(
        on_device,
        mesh=mesh,
        in_specs=(
            P("freq", "rec", None),
            P("freq", "rec", None),
            P("rec", "freq", None),
            P("rec", "freq", None),
            P("rec", None),
        ),
        out_specs=P("rec", "freq", None),
        check_vma=False,
    )
```

profile of v0, /device:TPU:0, one launch (start us, length us, event | category | flops | bytes accessed | tf_op | source)
XLA Modules:
  0.0 430.6 jit_solution(14480018314739985618)
XLA Ops:
  0.0 0.9 copy.13
  0.9 0.1 reshape.12.onset_ref
  1.0 0.0 copy-start.2
  1.0 0.6 constant_dynamic-slice_fusion.5
  1.7 0.8 constant_dynamic-slice_fusion.3
  2.4 0.6 pad_maximum_fusion.fh_ref
  3.0 0.8 constant_dynamic-slice_fusion.1
  3.8 0.6 pad_maximum_fusion.1.fl_ref
  4.4 0.0 copy-done.2
  4.4 187.9 %adjoint.1 = (f32[96,192,128]{2,1,0:T(8,128)}, s32[192,128]{1,0:T(8,128)}) custom-call(f32[4608,128]{1,0:T(8,128)} %bitcast.8, s32[96,128]{1,0:T(8,128)} %copy-done.2, f32[24,192,1536]{2,1,0:T(8,128)} %real_ref.3, f32[24,192,1536]{2,1,0:T(8,128)} %imag_ref.3), custom_call_target="tpu_custom_call" | custom-call | tf_op jit(solution)/shard_map/adjoint/pallas_call | solution.py:371
  192.3 1.4 constant_dynamic-slice_fusion
  193.7 26.7 %window.1.win_ref = f32[2,24,192,128]{3,2,1,0:T(8,128)} custom-call(s32[24,4,128]{2,1,0:T(4,128)} %bitcast.9, bf16[192,192]{1,0:T(8,128)(2,1)} %constant.59.clone.ih_ref, bf16[192,192]{1,0:T(8,128)(2,1)} %constant.60.clone.il_ref, bf16[96,192]{1,0:T(8,128)(2,1)} %pad_maximum_fusion.fh_ref, bf16[96,192]{1,0:T(8,128)(2,1)} %pad_maximum_fusion.1.fl_ref, ...), custom_call_target="tpu_custom_call" | custom-call | tf_op jit(solution)/shard_map/window/pallas_call | solution.py:691
  220.4 189.0 %forward.1.x_ref = f32[96,96,128]{2,1,0:T(8,128)} custom-call(f32[2,24,192,128]{3,2,1,0:T(8,128)} %window.1.win_ref, f32[24,192,1536]{2,1,0:T(8,128)} %real_ref.3, f32[24,192,1536]{2,1,0:T(8,128)} %imag_ref.3), custom_call_target="tpu_custom_call" | custom-call | tf_op jit(solution)/shard_map/forward/pallas_call | solution.py:610
  409.5 13.7 %window_rows.1 = f32[2,96,24,128]{3,2,1,0:T(8,128)} custom-call(s32[12,4,128]{2,1,0:T(4,128)} %bitcast.10, bf16[192,192]{1,0:T(8,128)(2,1)} %constant.59.clone.ih_ref, bf16[192,192]{1,0:T(8,128)(2,1)} %constant.60.clone.il_ref, bf16[96,192]{1,0:T(8,128)(2,1)} %pad_maximum_fusion.fh_ref, bf16[96,192]{1,0:T(8,128)(2,1)} %pad_maximum_fusion.1.fl_ref, ...), custom_call_target="tpu_custom_call" | custom-call | tf_op jit(solution)/shard_map/window_rows/pallas_call | solution.py:691
  423.2 0.0 copy-start
  423.2 2.5 dynamic-slice_bitcast_fusion
  425.7 0.4 collective-permute-start
  426.1 0.0 copy-start.1
  426.1 2.7 collective-permute-done
  428.8 0.0 copy-done
  428.8 0.2 bitcast_select_fusion.1
  428.9 0.0 copy-done.1
  429.0 1.6 maximum_subtract_fusion
Async XLA Ops:
  1.0 3.4 copy-start.2
  423.2 5.6 %copy-start = (f32[2,96,24,128]{3,2,1,0:T(8,128)S(1)}, f32[2,96,24,128]{3,2,1,0:T(8,128)}, u32[]{:S(2)}) copy-start(f32[2,96,24,128]{3,2,1,0:T(8,128)} %window_rows.1) | copy-start | bytes 7077892
  425.7 3.1 collective-permute-start
  426.1 2.9 copy-start.1
where the time goes:
time: 432 us; the launch traced here: 431 us
  Pallas kernels  417 us (97%)
  local copies, waits for them, and re-layouts  7.1 us (2%)
    pallas_call x1, Pallas kernels, forward(): pl.pallas_call(forward_kernel, out_shape=jax.ShapeDtypeStruct((p.FQ * nf,...  189 us
    pallas_call x1, Pallas kernels, adjoint(): pl.pallas_call(adjoint_kernel, out_shape=(jax.ShapeDtypeStruct((p.FQ * nf...  188 us
    pallas_call x2, Pallas kernels, window(): pl.pallas_call(functools.partial(window_kernel, by_row), grid=(count // r...  40.4 us
  transfers between devices with their start and end apart: 1, of which 1 were waited for; matrix products, arithmetic and copies ran while one was open for 0% of the time, Pallas kernels for 0%

commit v1 on v0

--- a/solution.py
+++ b/solution.py
@@ -66,6 +66,28 @@
     lax.fori_loop(0, count, lambda k, _: (body(k), 0)[1], 0)
 
 
+def partners(p):
+    found = [(p.z < p.Z - 1, p.above()), (p.z > 0, p.below())]
+    found += [(p.z >= 0, p.beside(dy)) for dy in range(1, p.Y)]
+    for step in range(1, p.FQ):
+        found.append((p.z >= 0, ((p.freq + step) % p.FQ, p.rec)))
+    return found
+
+
+def greet(found):
+    barrier = pltpu.get_barrier_semaphore()
+    for wanted, device in found:
+
+        @pl.when(wanted)
+        def _():
+            pl.semaphore_signal(barrier, inc=1, device_id=device, device_id_type=MESH)
+
+
+def meet(found):
+    total = sum(wanted.astype(jnp.int32) for wanted, _ in found)
+    pl.semaphore_wait(pltpu.get_barrier_semaphore(), total)
+
+
 def fetch_response(real_ref, imag_ref, buf, sems, f):
     slots = buf.shape[0]
     rows = buf.shape[1] // 2
@@ -76,44 +98,36 @@
     ]
 
 
-def spread(p, f, half, src, dst, own_sem, send, recv):
-    nf = dst.shape[0] // p.FQ
-    row = p.freq * nf + f
+def spread(p, half, src, dst, own, send, recv):
     for dx in range(p.X):
-        target = ((p.x + dx) % p.X * CORES + half, p.rec)
-        copy = remote(src, dst.at[row], send.at[half, dx, f], recv.at[p.freq, f], target)
+        copy = remote(src, dst, send(dx), recv, ((p.x + dx) % p.X * CORES + half, p.rec))
         if dx == 0:
-            mine = p.c == half
-
-            @pl.when(mine)
-            def _():
-                pltpu.make_async_copy(src, dst.at[row], own_sem.at[f]).start()
-
-            @pl.when(jnp.logical_not(mine))
+
+            @pl.when(p.c == half)
+            def _():
+                pltpu.make_async_copy(src, dst, own).start()
+
+            @pl.when(p.c != half)
             def _():
                 copy.start()
         else:
             copy.start()
 
 
-def spread_wait(p, f, src, dst, own_sem, send, recv):
-    nf = dst.shape[0] // p.FQ
-    pltpu.make_async_copy(src, dst.at[p.freq * nf + f], own_sem.at[f]).wait()
-    for half in range(CORES):
-        for dx in range(p.X):
-            copy = remote(src, dst.at[f], send.at[half, dx, f], recv.at[p.freq, f], (p.freq, p.rec))
-            if dx == 0:
-
-                @pl.when(p.c != half)
-                def _():
-                    copy.wait_send()
-            else:
+def spread_sent(p, half, src, dst, own, send):
+    for dx in range(p.X):
+        copy = remote(src, dst, send(dx), own, (p.freq, p.rec))
+        if dx == 0:
+
+            @pl.when(p.c == half)
+            def _():
+                pltpu.make_async_copy(src, dst, own).wait()
+
+            @pl.when(p.c != half)
+            def _():
                 copy.wait_send()
-    for source in range(p.FQ):
-
-        @pl.when(p.freq != source)
-        def _():
-            remote(src, dst.at[source * nf + f], send.at[0, 0, f], recv.at[source, f], (p.freq, p.rec)).wait_recv()
+        else:
+            copy.wait_send()
 
 
 def adjoint_kernel(focus_ref, onset_ref, real_ref, imag_ref, out_ref, own_onset_ref, *scratch):
@@ -127,32 +141,30 @@
     SR, SH = SU // SUBS, SU // CORES
     H = p.Z // 2
     U = 2 * Y
+    per_half = SUBS // CORES
     nr = buf.shape[1] // 2
     sign = jnp.where(lax.broadcasted_iota(jnp.int32, (1, width), 1) < width // 2, 1.0, -1.0)
 
     def fetch(f):
         return fetch_response(real_ref, imag_ref, buf, fetch_sem, f)
 
+    owner = p.rec // H
+    owner_rec = owner // Y * (p.Z - 1) * Y + owner % Y
+    onset_rows = onset_ref.shape[0]
+
+    def onset_copy(at):
+        dst = own_onset_ref.at[pl.ds(at * onset_rows, onset_rows)]
+        return remote(onset_ref, dst, so.at[0], qo.at[at], (p.freq, owner_rec))
+
+    found = partners(p)
+    found.append((owner_rec != p.rec, (p.freq, owner_rec)))
+    for at in range(H):
+        giver = p.unit * H + at
+        found.append((both(p.corner, giver != p.rec), (p.freq, giver)))
+    greet(found)
     for f in range(min(slots, nf)):
         for copy in fetch(f):
             copy.start()
-
-    owner = p.rec // H
-    owner_rec = owner // Y * (p.Z - 1) * Y + owner % Y
-    onset_rows = onset_ref.shape[0]
-
-    def onset_copy(at):
-        dst = own_onset_ref.at[pl.ds(at * onset_rows, onset_rows)]
-        return remote(onset_ref, dst, so.at[0], qo.at[at], (p.freq, owner_rec))
-
-    @pl.when(owner_rec == p.rec)
-    def _():
-        at = p.rec % H
-        pltpu.make_async_copy(onset_ref, own_onset_ref.at[pl.ds(at * onset_rows, onset_rows)], so.at[1]).start()
-
-    @pl.when(owner_rec != p.rec)
-    def _():
-        onset_copy(p.rec % H).start()
 
     def compute(f):
         for copy in fetch(f):
@@ -177,19 +189,15 @@
     def rows_of(k):
         return pl.ds(k % SUBS * SR, SR)
 
-    def halves(k):
-        return range(CORES) if SUBS == 1 else [k % SUBS]
+    def portion(f, sub):
+        half, at = sub // per_half, sub % per_half
+        src = term.at[f, p.end, p.y, pl.ds(sub * SR, SR)]
+        dst = out_ref.at[p.freq * nf + f, pl.ds(at * SR, SR)]
+        slot = f * per_half + at
+        return half, src, dst, own_sem.at[slot], lambda dx: sx.at[half, dx, slot], qx.at[p.freq, slot]
 
     def deliver(f, k):
-        if SUBS == 1:
-            for half in range(CORES):
-                spread(p, f, half, term.at[f, p.end, p.y, pl.ds(half * SH, SH)], out_ref, own_sem, sx, qx)
-        else:
-            for half in range(CORES):
-
-                @pl.when(k % SUBS == half)
-                def _():
-                    spread(p, f, half, term.at[f, p.end, p.y, pl.ds(half * SH, SH)], out_ref, own_sem, sx, qx)
+        spread(p, *portion(f, k % SUBS))
 
     def y_copy(k, dy):
         f = k // SUBS * 2
@@ -220,27 +228,37 @@
     hops = (p.down_hops, p.up_hops)
     thin_from, wide_from = (rd1, ru1), (rd2, ru2)
 
+    def begin(k):
+        for dy in range(1, Y):
+            y_copy(k, dy).start()
+        for end in range(2):
+
+            @pl.when(starts[end])
+            def _():
+                wide_copy(k, end).start()
+
+    compute(0)
+    compute(1)
+    meet(found)
+    @pl.when(owner_rec == p.rec)
+    def _():
+        at = p.rec % H
+        pltpu.make_async_copy(onset_ref, own_onset_ref.at[pl.ds(at * onset_rows, onset_rows)], so.at[1]).start()
+
+    @pl.when(owner_rec != p.rec)
+    def _():
+        onset_copy(p.rec % H).start()
+
+    begin(0)
+
     def step(i):
-        if SUBS == 1:
-            fresh = i < count
-        else:
-            fresh = both(i < count, i % SUBS == 0)
-
-        @pl.when(fresh)
-        def _():
-            f = i // SUBS * 2
-            compute(f)
-            compute(f + 1)
-
-        @pl.when(i < count)
-        def _():
-            for dy in range(1, Y):
-                y_copy(i, dy).start()
-            for end in range(2):
-
-                @pl.when(starts[end])
-                def _():
-                    wide_copy(i, end).start()
+        @pl.when(i + 2 < nf)
+        def _():
+            compute(i + 2)
+
+        @pl.when(i + 1 < count)
+        def _():
+            begin(i + 1)
 
         for end in range(2):
             k = i - hops[end]
@@ -320,7 +338,20 @@
 
     @pl.when(p.corner)
     def _():
-        loop(nf, lambda f: spread_wait(p, f, term.at[f, p.end, p.y, pl.ds(0, SH)], out_ref, own_sem, sx, qx))
+        def settle(f):
+            for sub in range(SUBS):
+                spread_sent(p, *portion(f, sub)[:-1])
+            for source in range(p.FQ):
+
+                @pl.when(p.freq != source)
+                def _():
+                    for at in range(per_half):
+                        src = term.at[f, p.end, p.y, pl.ds(0, SR)]
+                        dst = out_ref.at[source * nf + f, pl.ds(at * SR, SR)]
+                        slot = f * per_half + at
+                        remote(src, dst, sx.at[0, 0, slot], qx.at[source, slot], (p.freq, p.rec)).wait_recv()
+
+        loop(nf, settle)
         for at in range(H):
 
             @pl.when(p.unit * H + at != p.rec)
@@ -362,9 +393,9 @@
         *[dma((count,))] * 8,
         dma((count, Y - 1)),
         dma((count, Y - 1)),
-        dma((nf,)),
-        dma((CORES, p.X, nf)),
-        dma((p.FQ, nf)),
+        dma((nf * SUBS // CORES,)),
+        dma((CORES, p.X, nf * SUBS // CORES)),
+        dma((p.FQ, nf * SUBS // CORES)),
         dma((2,)),
         dma((H,)),
     ]
@@ -377,7 +408,9 @@
         in_specs=[IN_VMEM, ANY, ANY, ANY],
         out_specs=(ANY, ANY),
         scratch_shapes=scratch,
-        compiler_params=pltpu.CompilerParams(has_side_effects=True, vmem_limit_bytes=VMEM_LIMIT),
+        compiler_params=pltpu.CompilerParams(
+            collective_id=1, has_side_effects=True, vmem_limit_bytes=VMEM_LIMIT
+        ),
         name="adjoint",
     )(focus.reshape(nr * nf, width), onset_pairs, real, imag)
 
@@ -399,6 +432,8 @@
     def fetch(f):
         return fetch_response(real_ref, imag_ref, buf, fetch_sem, f)
 
+    found = partners(p)
+    greet(found)
     for f in range(min(slots, nf)):
         for copy in fetch(f):
             copy.start()
@@ -421,11 +456,13 @@
 
     @pl.when(p.corner)
     def _():
-        def begin(g):
-            core_copy(g).start()
-            own_copy(g).start()
-
-        loop(pairs, begin)
+        loop(pairs, lambda g: own_copy(g).start())
+
+    meet(found)
+
+    @pl.when(p.corner)
+    def _():
+        loop(pairs, lambda g: core_copy(g).start())
 
     def rows_of(k):
         return pl.ds(k % SUBS * SR, SR)
@@ -477,29 +514,39 @@
             for copy in fetch(f + slots):
                 copy.start()
 
+    def portion(f, half):
+        src = fo.at[f, pl.ds(half * NH, NH)]
+        dst = out_ref.at[p.freq * nf + f]
+        return half, src, dst, own_sem.at[f], lambda dx: sx.at[half, dx, f], qx.at[p.freq, f]
+
     def deliver(f):
         for half in range(CORES):
-            spread(p, f, half, fo.at[f, pl.ds(half * NH, NH)], out_ref, own_sem, sx, qx)
+            spread(p, *portion(f, half))
+
+    def begin(k):
+        for end in range(2):
+
+            @pl.when(starts[end])
+            def _():
+                for dy in range(1, Y):
+                    first_y(k, dy, end).start()
+                thin_copy(k, end).start()
+
+    @pl.when(p.corner)
+    def _():
+        own_copy(0).wait()
+        core_copy(0).wait_recv()
+        begin(0)
 
     def step(i):
-        @pl.when(both(p.corner, i < count))
-        def _():
-            if SUBS == 1:
-                fresh = i >= 0
-            else:
-                fresh = i % SUBS == 0
-
-            @pl.when(fresh)
-            def _():
-                own_copy(i // SUBS).wait()
-                core_copy(i // SUBS).wait_recv()
-
-            for end in range(2):
-
-                @pl.when(starts[end])
-                def _():
-                    for dy in range(1, Y):
-                        first_y(i, dy, end).start()
+        @pl.when(both(p.corner, i + 1 < count))
+        def _():
+            @pl.when((i + 1) % SUBS == 0)
+            def _():
+                own_copy((i + 1) // SUBS).wait()
+                core_copy((i + 1) // SUBS).wait_recv()
+
+            begin(i + 1)
 
         for end in range(2):
             k = i - hops[end]
@@ -510,7 +557,7 @@
                 def _():
                     thin_copy(k, end).wait_recv()
 
-                @pl.when(jnp.logical_not(stops[end]))
+                @pl.when(jnp.logical_not(jnp.logical_or(starts[end], stops[end])))
                 def _():
                     thin_copy(k, end).start()
 
@@ -542,20 +589,14 @@
                 for dy in range(1, Y):
                     last_y(k, dy, end).wait_recv()
 
-            if SUBS == 1:
-                ready = k >= 0
-            else:
-                ready = k % SUBS == SUBS - 1
-
-            @pl.when(ready)
-            def _():
-                f = k // SUBS * 2
-                compute(f)
-                deliver(f)
-                compute(f + 1)
-                deliver(f + 1)
-
-    loop(count + p.Z, step)
+        f = k - SUBS + 1
+
+        @pl.when(within(f, nf))
+        def _():
+            compute(f)
+            deliver(f)
+
+    loop(count + p.Z + SUBS - 1, step)
 
     def finish(k):
         for end in range(2):
@@ -578,7 +619,18 @@
     def _():
         loop(pairs, lambda g: core_copy(g).wait_send())
 
-    loop(nf, lambda f: spread_wait(p, f, fo.at[f, pl.ds(0, NH)], out_ref, own_sem, sx, qx))
+    def settle(f):
+        for half in range(CORES):
+            spread_sent(p, *portion(f, half)[:-1])
+        for source in range(p.FQ):
+
+            @pl.when(p.freq != source)
+            def _():
+                src = fo.at[f, pl.ds(0, NH)]
+                dst = out_ref.at[source * nf + f]
+                remote(src, dst, sx.at[0, 0, f], qx.at[source, f], (p.freq, p.rec)).wait_recv()
+
+    loop(nf, settle)
 
 
 def forward(windowed, real, imag):
@@ -613,18 +665,20 @@
         in_specs=[ANY, ANY, ANY],
         out_specs=ANY,
         scratch_shapes=scratch,
-        compiler_params=pltpu.CompilerParams(has_side_effects=True, vmem_limit_bytes=VMEM_LIMIT),
+        compiler_params=pltpu.CompilerParams(
+            collective_id=2, has_side_effects=True, vmem_limit_bytes=VMEM_LIMIT
+        ),
         name="forward",
     )(windowed, real, imag)
 
 
-def split_host(table):
+def stack_host(table):
     high = np.asarray(table, dtype=jnp.bfloat16)
     low = np.asarray(table - high.astype(np.float64), dtype=jnp.bfloat16)
-    return high, low
-
-
-def tables(freqs):
+    return np.concatenate([high, low], axis=-2)
+
+
+def tables(freqs, chips):
     samples = 2 * freqs
     order = np.arange(freqs)
     sample = np.arange(samples)
@@ -632,74 +686,163 @@
     cosine, sine = np.cos(phases), np.sin(phases)
     factor = np.where(order == 0, 1.0, 2.0)[:, None] / samples
     inverse = np.concatenate([(factor * cosine).T, (-factor * sine).T], axis=1)
-    return (*split_host(inverse), *split_host(cosine), *split_host(-sine))
-
-
-def triple(high, low, x):
-    x_high, x_low = split(x)
+    shape = (chips, freqs // chips, samples)
+    forward = np.concatenate([cosine.reshape(shape), -sine.reshape(shape)], axis=1)
+    return jnp.asarray(stack_host(inverse)), jnp.asarray(stack_host(forward))
+
+
+def triple(stack, x):
+    high, low = split(x)
     dot = functools.partial(jnp.dot, preferred_element_type=jnp.float32)
-    return dot(high, x_high) + (dot(high, x_low) + dot(low, x_high))
-
-
-def window_kernel(by_row, onset_ref, ih_ref, il_ref, fh_ref, fl_ref, x_ref, o_ref):
-    freqs, rows, width = x_ref.shape
+    rows = stack.shape[0] // 2
+    wide = dot(stack, high)
+    return wide[:rows] + (wide[rows:] + dot(stack[:rows], low))
+
+
+def window_rows(inverse, forward, onset_ref, x_ref, start, count, store):
+    freqs, _, width = x_ref.shape
+    half = width // 2
     samples = 2 * freqs
-    half = width // 2
-    kept = fh_ref.shape[0] // 2
-    own = kept // CORES
+    kept = forward.shape[0] // 4
+    pairs = count // 2
     first = lax.broadcasted_iota(jnp.int32, (1, width), 1) < half
     sample = lax.broadcasted_iota(jnp.int32, (samples, width), 0)
-    pairs = rows // 2
     packed = []
     for i in range(pairs):
-        a, b = x_ref[:, 2 * i, :], x_ref[:, 2 * i + 1, :]
+        a, b = x_ref[:, start + 2 * i, :], x_ref[:, start + 2 * i + 1, :]
         real = jnp.where(first, a, pltpu.roll(b, half, 1))
         imag = jnp.where(first, pltpu.roll(a, half, 1), b)
         packed.append(jnp.concatenate([real, imag], axis=0))
-    traces = triple(ih_ref[...], il_ref[...], jnp.concatenate(packed, axis=1))
-    clipped = [
-        jnp.where(sample < onset_ref[0, i : i + 1, :], traces[:, i * width : (i + 1) * width], 0.0)
-        for i in range(pairs)
-    ]
-    back = triple(fh_ref[...], fl_ref[...], jnp.concatenate(clipped, axis=1))
+    traces = triple(inverse, jnp.concatenate(packed, axis=1))
+    clipped = []
+    for i in range(pairs):
+        onset = onset_ref[start // 2 + i : start // 2 + i + 1, :]
+        clipped.append(jnp.where(sample < onset, traces[:, i * width : (i + 1) * width], 0.0))
+    back = triple(forward, jnp.concatenate(clipped, axis=1))
     for i in range(pairs):
         real = back[:kept, i * width : (i + 1) * width]
         imag = back[kept:, i * width : (i + 1) * width]
-        a = jnp.where(first, real, pltpu.roll(imag, half, 1))
-        b = jnp.where(first, pltpu.roll(real, half, 1), imag)
-        for n, value in ((2 * i, a), (2 * i + 1, b)):
-            for core in range(CORES):
-                piece = value[core * own : (core + 1) * own]
-                if by_row:
-                    o_ref[core, n] = piece
-                else:
-                    o_ref[core, :, n, :] = piece
-
-
-def window(spectrum, onset_pairs, consts, by_row):
+        store(start + 2 * i, jnp.where(first, real, pltpu.roll(imag, half, 1)))
+        store(start + 2 * i + 1, jnp.where(first, pltpu.roll(real, half, 1), imag))
+
+
+def groups(rows):
+    step = 16 if rows % 16 == 0 else 8
+    return [(start, step) for start in range(0, rows, step)]
+
+
+def rows_per_step(count):
+    for rows in (48, 32):
+        if count % rows == 0:
+            return rows
+    return 8
+
+
+def source_window_kernel(onset_ref, inverse_ref, forward_ref, x_ref, o_ref):
+    p = Place()
+    rows = x_ref.shape[1]
+    own = o_ref.shape[1]
+    onsets = onset_ref.at[p.c * pl.num_programs(0) + pl.program_id(0)]
+    inverse, forward_table = inverse_ref[...], forward_ref[p.x]
+
+    def store(n, value):
+        for core in range(CORES):
+            o_ref[core, :, n, :] = value[core * own : (core + 1) * own]
+
+    for start, count in groups(rows):
+        window_rows(inverse, forward_table, onsets, x_ref, start, count, store)
+
+
+def source_window(spectrum, onset_pairs, inverse, forward_table):
     freqs, count, width = spectrum.shape
-    own = consts[2].shape[0] // 2 // CORES
-    rows = 8
-    onset_pairs = onset_pairs.reshape(count // rows, rows // 2, width)
-    whole = [pl.BlockSpec(t.shape, lambda i: (0, 0)) for t in consts]
-    if by_row:
-        out_shape, out_block = (CORES, count, own, width), (CORES, rows, own, width)
-        out_spec = pl.BlockSpec(out_block, lambda i: (0, i, 0, 0))
-    else:
-        out_shape, out_block = (CORES, own, count, width), (CORES, own, rows, width)
-        out_spec = pl.BlockSpec(out_block, lambda i: (0, 0, i, 0))
+    own = forward_table.shape[1] // 4 // CORES
+    rows = rows_per_step(count)
+    steps = count // rows
+    onset_pairs = onset_pairs.reshape(CORES * steps, rows // 2, width)
     return pl.pallas_call(
-        functools.partial(window_kernel, by_row),
-        grid=(count // rows,),
+        source_window_kernel,
+        grid=(steps,),
         in_specs=[
-            pl.BlockSpec((1, rows // 2, width), lambda i: (i, 0, 0)),
-            *whole,
+            *[IN_VMEM] * 3,
             pl.BlockSpec((freqs, rows, width), lambda i: (0, i, 0)),
         ],
-        out_specs=out_spec,
-        out_shape=jax.ShapeDtypeStruct(out_shape, jnp.float32),
-        name="window_rows" if by_row else "window",
-    )(onset_pairs, *consts, spectrum)
+        out_specs=pl.BlockSpec((CORES, own, rows, width), lambda i: (0, 0, i, 0)),
+        out_shape=jax.ShapeDtypeStruct((CORES, own, count, width), jnp.float32),
+        compiler_params=pltpu.CompilerParams(vmem_limit_bytes=VMEM_LIMIT),
+        name="source_window",
+    )(onset_pairs, inverse, forward_table, spectrum)
+
+
+def receiver_window_kernel(onset_ref, inverse_ref, forward_ref, x_ref, o_ref, buf, give, sb, ss, qs):
+    p = Place()
+    steps, rows, nf, _ = give.shape
+    count = steps * rows
+    other = (p.x * CORES + 1 - p.c, p.rec)
+    barrier = pltpu.get_barrier_semaphore()
+    pl.semaphore_signal(barrier, inc=1, device_id=other, device_id_type=MESH)
+
+    def block(i):
+        slot = i % 2
+        src = x_ref.at[:, pl.ds(i * rows, rows)]
+        return pltpu.make_async_copy(src, buf.at[slot], sb.at[slot])
+
+    def give_copy(i):
+        dst = o_ref.at[pl.ds(p.c * count + i * rows, rows)]
+        return remote(give.at[i], dst, ss.at[i], qs.at[i], other)
+
+    block(0).start()
+    pl.semaphore_wait(barrier, 1)
+
+    def step(i):
+        @pl.when(i + 1 < steps)
+        def _():
+            block(i + 1).start()
+
+        block(i).wait()
+        inverse, forward_table = inverse_ref[...], forward_ref[p.x]
+        onsets = onset_ref.at[p.c * steps + i]
+        base = p.c * count + i * rows
+
+        def store(n, value):
+            o_ref[base + n] = jnp.where(p.c == 0, value[:nf], value[nf:])
+            give[i, n] = jnp.where(p.c == 0, value[nf:], value[:nf])
+
+        for start, size in groups(rows):
+            window_rows(inverse, forward_table, onsets, buf.at[i % 2], start, size, store)
+        give_copy(i).start()
+
+    loop(steps, step)
+
+    def settle(i):
+        give_copy(i).wait()
+
+    loop(steps, settle)
+
+
+def receiver_window(spectrum, onset_pairs, inverse, forward_table):
+    freqs, count, width = spectrum.shape
+    nf = forward_table.shape[1] // 4 // CORES
+    rows = rows_per_step(count)
+    steps = count // rows
+    onset_pairs = onset_pairs.reshape(CORES * steps, rows // 2, width)
+    dma = pltpu.SemaphoreType.DMA
+    return pl.pallas_call(
+        receiver_window_kernel,
+        in_specs=[*[IN_VMEM] * 3, ANY],
+        out_specs=IN_VMEM,
+        out_shape=jax.ShapeDtypeStruct((CORES * count, nf, width), jnp.float32),
+        scratch_shapes=[
+            pltpu.VMEM((2, freqs, rows, width), jnp.float32),
+            pltpu.VMEM((steps, rows, nf, width), jnp.float32),
+            dma((2,)),
+            dma((steps,)),
+            dma((steps,)),
+        ],
+        compiler_params=pltpu.CompilerParams(
+            collective_id=0, has_side_effects=True, vmem_limit_bytes=VMEM_LIMIT
+        ),
+        name="receiver_window",
+    )(onset_pairs, inverse, forward_table, spectrum)
 
 
 def on_device(response_real, response_imaginary, focus, initial, onset):
@@ -707,31 +850,11 @@
     nf, nr, _ = response_real.shape
     width = focus.shape[2]
     onset_pairs = onset.reshape(nr // 2, width)
-
-    inv_high, inv_low, cos_high, cos_low, sin_high, sin_low = tables(p.FQ * nf)
-
-    def chip_rows(cosine, sine):
-        at = p.x * CORES * nf
-        cut = [lax.dynamic_slice_in_dim(jnp.asarray(t), at, CORES * nf, 0) for t in (cosine, sine)]
-        return jnp.concatenate(cut, axis=0)
-
-    consts = [jnp.asarray(inv_high), jnp.asarray(inv_low), chip_rows(cos_high, sin_high), chip_rows(cos_low, sin_low)]
-
+    inverse, forward_table = tables(p.FQ * nf, p.X)
     spectrum, own_onset = adjoint(focus, onset_pairs, response_real, response_imaginary)
-    SH = spectrum.shape[1]
-    mine = lax.dynamic_slice_in_dim(own_onset, p.c * (SH // 2), SH // 2, 0)
-    windowed = window(spectrum, mine, consts, False)
+    windowed = source_window(spectrum, own_onset, inverse, forward_table)
     received = forward(windowed, response_real, response_imaginary)
-    quarter = nr // CORES // 2
-    mine = lax.dynamic_slice_in_dim(onset_pairs, p.c * quarter, quarter, 0)
-    update = window(received, mine, consts, True)
-    keep = lax.dynamic_index_in_dim(update, p.c, 0, keepdims=False)
-    give = lax.dynamic_index_in_dim(update, 1 - p.c, 0, keepdims=False)
-    swap = [(i, i ^ 1) for i in range(p.FQ)]
-    got = lax.ppermute(give, "freq", swap)
-    low = jnp.where(p.c == 0, keep, got)
-    high = jnp.where(p.c == 0, got, keep)
-    return initial - jnp.concatenate([low, high], axis=0)
+    return initial - receiver_window(received, onset_pairs, inverse, forward_table)
 
 
 def solution(mesh):

time: 432 us -> 407 us (0.942)
  Pallas kernels: 417 us -> 400 us
  local copies, waits for them, and re-layouts: 7.1 us -> 2.33 us
    pallas_call x2, Pallas kernels: 40.4 us -> 29.1 us  [the longest x1 17 us: source_window(): pl.pallas_call(source_window_kernel, grid=(steps,), in_specs=[*[IN_VMEM]...]
  transfers between devices with their start and end apart: 1 -> 0, of which waited for: 1 -> 0; matrix products, arithmetic and copies ran while one was open for 0% -> 0% of each run, Pallas kernels for 0% -> 0%
where the time goes in v1:
time: 407 us
  Pallas kernels  400 us (98%)
    pallas_call x1, Pallas kernels, forward(): pl.pallas_call(forward_kernel, out_shape=jax.ShapeDtypeStruct((p.FQ * nf,...  187 us
    pallas_call x1, Pallas kernels, adjoint(): pl.pallas_call(adjoint_kernel, out_shape=(jax.ShapeDtypeStruct((p.FQ * nf...  184 us
    pallas_call x1, Pallas kernels, source_window(): pl.pallas_call(source_window_kernel, grid=(steps,), in_specs=[*[IN_VMEM]...  17 us
    pallas_call x1, Pallas kernels, receiver_window(): pl.pallas_call(receiver_window_kernel, in_specs=[*[IN_VMEM] * 3, ANY], ou...  12.1 us

profile of v1, /device:TPU:0, one launch (start us, length us, event | category | flops | bytes accessed | tf_op | source)
XLA Modules:
  0.0 406.8 jit_solution(10079558512244028712)
XLA Ops:
  0.0 0.9 copy.10
  0.9 0.7 reshape.10.onset_ref
  1.6 0.7 reshape_reshape.3.onset_ref
  2.3 184.1 %adjoint.1 = (f32[96,192,128]{2,1,0:T(8,128)}, s32[192,128]{1,0:T(8,128)}) custom-call(f32[4608,128]{1,0:T(8,128)} %bitcast.2, s32[96,128]{1,0:T(8,128)} %reshape.10.onset_ref, f32[24,192,1536]{2,1,0:T(8,128)} %real_ref.3, f32[24,192,1536]{2,1,0:T(8,128)} %imag_ref.3), custom_call_target="tpu_custom_call" | custom-call | tf_op jit(solution)/shard_map/adjoint/pallas_call | solution.py:402
  186.4 17.0 %source_window.1.win_ref = f32[2,24,192,128]{3,2,1,0:T(8,128)} custom-call(s32[8,24,128]{2,1,0:T(8,128)} %bitcast.3, bf16[384,192]{1,0:T(8,128)(2,1)} %constant.4.clone.inverse_ref, bf16[2,192,192]{2,1,0:T(8,128)(2,1)} %constant.5.clone.forward_ref, f32[96,192,128]{2,1,0:T(8,128)} %get-tuple-element.8.x_ref), custom_call_target="tpu_custom_call" | custom-call | tf_op jit(solution)/shard_map/source_window/pallas_call | solution.py:762
  203.4 187.1 %forward.1.x_ref = f32[96,96,128]{2,1,0:T(8,128)} custom-call(f32[2,24,192,128]{3,2,1,0:T(8,128)} %source_window.1.win_ref, f32[24,192,1536]{2,1,0:T(8,128)} %real_ref.3, f32[24,192,1536]{2,1,0:T(8,128)} %imag_ref.3), custom_call_target="tpu_custom_call" | custom-call | tf_op jit(solution)/shard_map/forward/pallas_call | solution.py:662
  390.6 12.1 %receiver_window.1 = f32[192,24,128]{2,1,0:T(8,128)} custom-call(s32[4,24,128]{2,1,0:T(8,128)} %reshape_reshape.3.onset_ref, bf16[384,192]{1,0:T(8,128)(2,1)} %constant.4.clone.inverse_ref, bf16[2,192,192]{2,1,0:T(8,128)(2,1)} %constant.5.clone.forward_ref, f32[96,96,128]{2,1,0:T(8,128)} %forward.1.x_ref), custom_call_target="tpu_custom_call" | custom-call | tf_op jit(solution)/shard_map/receiver_window/pallas_call | solution.py:829
  402.7 4.0 sub.3
